TPU v7x, 32 devices: a whole 2x2x4 slice. The times are simulated.
32 devices in a mesh: band: 8 (over y, x, core), gblk: 4 (over z).
Axes of the slice: x: 2, y: 2, z: 4, core: 2. Of those that a mesh axis runs over, the one named last changes fastest.
Arguments:
- eps_inv: bfloat16 [2, 2, 8, 4, 512, 16384], P(None, None, None, 'gblk', None, 'band'), may hold values from -6 to 6
- pair_elements: bfloat16 [2, 1, 16, 16384], P(None, None, 'band'), may hold values from -0.046875 to 0.046875
Outputs:
- sigma_terms: float32 [2, 2, 1, 16], P(None, None, None, 'band')
All inputs are finite; a program needn't handle non-finite values.
Results may differ from a plain program's by a relative error of at most 0.0003.
Values may be sent and summed in bfloat16 or wider, within the bound.
No kernel may reach another device: no remote copies, remote signals or barrier semaphores. Data moves between devices by JAX's collectives and lax.ppermute only.
A program may use at most 128 MiB of HBM per device.

v0:
```python
import jax
import jax.numpy as jnp
from jax import lax
from jax.sharding import PartitionSpec as P


def shards(eps_inv, pair_elements):
    group_count = lax.axis_size("gblk")
    group_index = lax.axis_index("gblk")
    freqs = eps_inv.shape[0]
    rounds = eps_inv.shape[2]
    tile_rows = eps_inv.shape[4]
    width = eps_inv.shape[5]
    states = pair_elements.shape[1]
    local_bands = pair_elements.shape[2]
    columns = lax.all_to_all(pair_elements, "band", split_axis=3, concat_axis=2, tiled=True)
    all_bands = columns.shape[2]
    blocks = eps_inv.reshape(freqs, 2, -1, width)
    shaped = pair_elements.reshape(2, states, local_bands, rounds, group_count, tile_rows)
    picked = lax.dynamic_slice_in_dim(shaped, group_index, 1, 4)
    row_local = picked.reshape(2, states, local_bands, rounds * tile_rows)
    flat = columns.reshape(-1, width)
    contract_last = (((1,), (1,)), ((), ()))
    images = []
    for frequency in range(freqs):
        along_a = lax.dot_general(
            flat, blocks[frequency, 0], contract_last, preferred_element_type=jnp.float32
        )
        along_b = lax.dot_general(
            flat, blocks[frequency, 1], contract_last, preferred_element_type=jnp.float32
        )
        along_a = along_a.reshape(2, states, all_bands, -1)
        along_b = along_b.reshape(2, states, all_bands, -1)
        images.append(jnp.stack([along_a[0] - along_b[1], along_a[1] + along_b[0]]))
    image = jnp.stack(images)
    piece = lax.all_gather(row_local, "band", axis=2, tiled=True)
    real_part = piece[0].astype(jnp.float32)
    imag_part = piece[1].astype(jnp.float32)
    sigma_re = jnp.sum(real_part * image[:, 0] + imag_part * image[:, 1], axis=-1)
    sigma_im = jnp.sum(real_part * image[:, 1] - imag_part * image[:, 0], axis=-1)
    partial_sigma = jnp.stack([sigma_re, sigma_im], axis=1)
    reduced = lax.psum_scatter(partial_sigma, "band", scatter_dimension=3, tiled=True)
    return lax.psum(reduced, "gblk")


def solution(mesh):
    placed = (P(None, None, None, "gblk", None, "band"), P(None, None, "band", None))
    return jax.shard_map(
        shards, mesh=mesh, in_specs=placed, out_specs=P(None, None, None, "band"), check_vma=False
    )
```

profile of v0, /device:TPU:0, one launch (start us, length us, event | category | flops | bytes accessed | tf_op | source)
XLA Modules:
  0.0 138.5 jit_solution(16395664978475546550)
XLA Ops:
  0.0 0.0 copy-start.1
  0.0 0.0 copy-start
  0.0 15.4 %copy.24 = bf16[2,1,2,16384]{2,0,1,3:T(2,128)(2,1)} copy(bf16[2,1,2,16384]{3,2,1,0:T(2,128)(2,1)} %param.3) | data formatting | bytes 262144 | tf_op args[1]
  15.5 13.7 %reshape.124 = bf16[8,2,4096]{2,1,0:T(2,128)(2,1)} reshape(bf16[16384,1,2,2]{3,2,1,0:T(2,128)(2,1)} %bitcast.63) | data formatting | bytes 262144
  29.2 5.2 %all-to-all-start = ((bf16[8,2,4096]{2,1,0:T(2,128)(2,1)}), bf16[8,2,4096]{2,1,0:T(2,128)(2,1)S(1)}, u32[]{:S(2)}, u32[]{:S(2)}) async-start(bf16[8,2,4096]{2,1,0:T(2,128)(2,1)} %reshape.124), calls=%async_computation | async-start | bytes 262144 | tf_op jit(solution)/shard_map/all_to_all | solution.py:16
  34.4 0.0 copy-done
  34.4 0.1 reshape.113
  34.5 0.2 dynamic-slice_reduce_fusion
  34.8 9.8 %all_gather.3 = bf16[2,1,16,4096]{3,0,1,2:T(2,128)(2,1)S(1)} all-gather(bf16[2,1,2,4096]{3,0,1,2:T(2,128)(2,1)S(1)} %copy.23), channel_id=1, replica_groups=mesh['band'=8,'gblk'=4] {'band'}, dimensions={2}, use_global_device_ids=true | all-gather | bytes 294912 | tf_op jit(solution)/shard_map/all_gather | solution.py:36
  44.6 0.5 slice_convert_fusion.1
  45.1 0.3 copy_bitcast_fusion
  45.4 0.0 copy-done.1
  45.4 0.6 dynamic-slice
  46.7 0.0 all-to-all-done
  46.7 19.1 %reshape.125 = bf16[16384,1,2,2]{3,2,1,0:T(2,128)(2,1)} reshape(bf16[8,2,4096]{2,1,0:T(2,128)(2,1)S(1)} %all-to-all-done) | data formatting | bytes 262144
  65.8 11.9 %copy.29 = bf16[2,1,2,8,2048]{4,3,2,0,1:T(8,128)(2,1)S(1)} copy(bf16[2,1,2,8,2048]{2,0,4,3,1:T(2,128)(2,1)} %bitcast.62) | data formatting | bytes 262144 | tf_op jit(solution)/shard_map/all_to_all | solution.py:16
  77.6 0.1 copy.26
  77.8 0.1 reshape.115
  77.9 8.6 %fusion.2 = f32[32,4096]{1,0:T(8,128)S(1)} fusion(bf16[32,2048]{1,0:T(8,128)(2,1)S(1)} %reshape.115, bf16[2,2,4096,2048]{3,2,1,0:T(8,128)(2,1)} %bitcast.2), kind=kOutput, calls=%fused_computation.5 | convolution fusion | flops 536870912 | bytes 17432576 | tf_op jit(solution)/shard_map/dot_general | solution.py:29
  86.4 8.6 %fusion.3 = f32[32,4096]{1,0:T(8,128)S(1)} fusion(bf16[32,2048]{1,0:T(8,128)(2,1)S(1)} %reshape.115, bf16[2,2,4096,2048]{3,2,1,0:T(8,128)(2,1)} %bitcast.2), kind=kOutput, calls=%fused_computation.7 | convolution fusion | flops 536870912 | bytes 17432576 | tf_op jit(solution)/shard_map/dot_general | solution.py:26
  95.0 8.6 %fusion = f32[32,4096]{1,0:T(8,128)S(1)} fusion(bf16[32,2048]{1,0:T(8,128)(2,1)S(1)} %reshape.115, bf16[2,2,4096,2048]{3,2,1,0:T(8,128)(2,1)} %bitcast.2), kind=kOutput, calls=%fused_computation.1 | convolution fusion | flops 536870912 | bytes 17432576 | tf_op jit(solution)/shard_map/dot_general | solution.py:29
  103.6 8.6 %fusion.1 = f32[32,4096]{1,0:T(8,128)S(1)} fusion(bf16[32,2048]{1,0:T(8,128)(2,1)S(1)} %reshape.115, bf16[2,2,4096,2048]{3,2,1,0:T(8,128)(2,1)} %bitcast.2), kind=kOutput, calls=%fused_computation.3 | convolution fusion | flops 536870912 | bytes 17432576 | tf_op jit(solution)/shard_map/dot_general | solution.py:26
  112.2 0.1 fusion.10
  112.3 0.1 fusion.8
  112.4 0.2 add_reduce_fusion
  112.7 13.2 %all-reduce = f32[2,2,1,16]{3,0,2,1:T(2,128)S(1)} all-reduce(f32[2,2,1,16]{3,0,2,1:T(2,128)S(1)} %pad_maximum_fusion.1), channel_id=2, replica_groups=mesh['band'=8,'gblk'=4] {'band'}, use_global_device_ids=true, to_apply=%region_2.0.clone | all-reduce | flops 64 | bytes 512
  125.9 0.1 constant_dynamic-slice_fusion
  125.9 11.9 %psum.7 = f32[2,2,1,2]{3,0,2,1:T(2,128)S(1)} all-reduce(f32[2,2,1,2]{3,0,2,1:T(2,128)S(1)} %constant_dynamic-slice_fusion), channel_id=1, replica_groups=mesh['band'=8,'gblk'=4] {'gblk'}, use_global_device_ids=true, to_apply=%region_3.0 | all-reduce | flops 8 | bytes 64 | tf_op jit(solution)/shard_map/psum | solution.py:43
  137.9 0.6 copy.28
  (5 shorter events, 0.1 us)
Async XLA Ops:
  0.0 45.4 %copy-start.1 = (u32[32]{0:T(128)S(1)}, u32[32]{0:T(128)}, u32[]{:S(2)}) copy-start(u32[32]{0:T(128)} %constant.14) | copy-start | bytes 388
  0.0 34.4 %copy-start = (bf16[2,1,2,16384]{3,2,1,0:T(2,128)(2,1)S(1)}, bf16[2,1,2,16384]{3,2,1,0:T(2,128)(2,1)}, u32[]{:S(2)}) copy-start(bf16[2,1,2,16384]{3,2,1,0:T(2,128)(2,1)} %param.3) | copy-start | bytes 393220
  29.2 17.5 %all-to-all-start = ((bf16[8,2,4096]{2,1,0:T(2,128)(2,1)}), bf16[8,2,4096]{2,1,0:T(2,128)(2,1)S(1)}, u32[]{:S(2)}, u32[]{:S(2)}) async-start(bf16[8,2,4096]{2,1,0:T(2,128)(2,1)} %reshape.124), calls=%async_computation | async-start | bytes 262144 | tf_op jit(solution)/shard_map/all_to_all | solution.py:16
where the time goes:
time: 140 us; the launch traced here: 138 us
  local copies, waits for them, and re-layouts  62.2 us (44%)
  blocking collectives  35 us (25%)
  matrix products  34.3 us (24%)
  starting transfers between devices  5.2 us (4%)
    unnamed x10, local copies, waits for them, and re-layouts  49.2 us
    dot_general x2, matrix products, shards(): lax.dot_general(flat, blocks[frequency, 0], contract_last, preferred_elem...  17.2 us
    dot_general x2, matrix products, shards(): lax.dot_general(flat, blocks[frequency, 1], contract_last, preferred_elem...  17.1 us
    unnamed x1, blocking collectives  13.2 us
    all_to_all x2, local copies, waits for them, and re-layouts, shards(): lax.all_to_all(pair_elements, 'band', split_axis=3, concat_axis=2, tiled=...  12 us
    psum x1, blocking collectives, shards(): return lax.psum(reduced, 'gblk')  11.9 us
    all_gather x1, blocking collectives, shards(): piece = lax.all_gather(row_local, 'band', axis=2, tiled=True)  9.81 us
    all_to_all x1, starting transfers between devices, shards(): lax.all_to_all(pair_elements, 'band', split_axis=3, concat_axis=2, tiled=...  5.2 us
  transfers between devices with their start and end apart: 1, of which 0 were waited for; matrix products, arithmetic and copies ran while one was open for 1% of the time, Pallas kernels for 0%

commit v1 on v0

--- a/solution.py
+++ b/solution.py
@@ -2,6 +2,17 @@
 import jax.numpy as jnp
 from jax import lax
 from jax.sharding import PartitionSpec as P
+
+
+def split_up(x, dim, size):
+    before, after = (x.shape[:dim], x.shape[dim + 1 :])
+    return jnp.moveaxis(x.reshape(*before, size, -1, *after), dim, 0)
+
+
+def laid_out(parts, dim):
+    parts = jnp.moveaxis(parts, 0, dim)
+    shape = parts.shape
+    return parts.reshape(*shape[:dim], shape[dim] * shape[dim + 1], *shape[dim + 2 :])
 
 
 def shards(eps_inv, pair_elements):
@@ -13,7 +24,14 @@
     width = eps_inv.shape[5]
     states = pair_elements.shape[1]
     local_bands = pair_elements.shape[2]
-    columns = lax.all_to_all(pair_elements, "band", split_axis=3, concat_axis=2, tiled=True)
+    count, index = (lax.axis_size("band"), lax.axis_index("band"))
+    blocks_2 = split_up(pair_elements, 3, count)
+    outs = [blocks_2[index]]
+    for step in range(1, count):
+        sent = blocks_2[index ^ step]
+        outs.append(lax.ppermute(sent, "band", [(i, i ^ step) for i in range(count)]))
+    blocks_2 = jnp.stack(outs)[index ^ jnp.arange(count)]
+    columns = laid_out(blocks_2, 2)
     all_bands = columns.shape[2]
     blocks = eps_inv.reshape(freqs, 2, -1, width)
     shaped = pair_elements.reshape(2, states, local_bands, rounds, group_count, tile_rows)

time: 140 us -> 87.5 us (0.62)
  local copies, waits for them, and re-layouts: 62.2 us -> 6.02 us
  waiting for transfers between devices: 0.01 us -> 2.79 us
  starting transfers between devices: 5.2 us -> 7.92 us
    unnamed x10 -> x17, local copies, waits for them, and re-layouts: 49.2 us -> 1.9 us
    all_to_all x2 -> x0, local copies, waits for them, and re-layouts: 12 us -> none  [shards(): lax.all_to_all(pair_elements, 'band', split_axis=3, concat_axis=2, tiled=...]
    ppermute x0 -> x7, starting transfers between devices: none -> 7.92 us  [shards(): lax.ppermute(sent, 'band', [(i, i ^ step) for i in range(count)])]
    all_to_all x1 -> x0, starting transfers between devices: 5.2 us -> none  [shards(): lax.all_to_all(pair_elements, 'band', split_axis=3, concat_axis=2, tiled=...]
    ppermute x0 -> x7, waiting for transfers between devices: none -> 2.79 us  [shards(): lax.ppermute(sent, 'band', [(i, i ^ step) for i in range(count)])]
  transfers between devices with their start and end apart: 1 -> 7, of which waited for: 0 -> 2; matrix products, arithmetic and copies ran while one was open for 1% -> 4% of each run, Pallas kernels for 0% -> 0%
where the time goes in v1:
time: 87.5 us; the launch traced here: 87.3 us
  blocking collectives  34.3 us (39%)
  matrix products  34.3 us (39%)
  starting transfers between devices  7.92 us (9%)
  local copies, waits for them, and re-layouts  6.02 us (7%)
  waiting for transfers between devices  2.79 us (3%)
  other arithmetic  1.02 us (1%)
  between operations  0.92 us (1%)
    dot_general x2, matrix products, shards(): lax.dot_general(flat, blocks[frequency, 0], contract_last, preferred_elem...  17.2 us
    dot_general x2, matrix products, shards(): lax.dot_general(flat, blocks[frequency, 1], contract_last, preferred_elem...  17.1 us
    unnamed x1, blocking collectives  13 us
    psum x1, blocking collectives, shards(): return lax.psum(reduced, 'gblk')  11.9 us
    all_gather x1, blocking collectives, shards(): piece = lax.all_gather(row_local, 'band', axis=2, tiled=True)  9.42 us
    ppermute x7, starting transfers between devices, shards(): lax.ppermute(sent, 'band', [(i, i ^ step) for i in range(count)])  7.92 us
    ppermute x7, waiting for transfers between devices, shards(): lax.ppermute(sent, 'band', [(i, i ^ step) for i in range(count)])  2.79 us
    unnamed x17, local copies, waits for them, and re-layouts  1.9 us
  transfers between devices with their start and end apart: 7, of which 2 were waited for; matrix products, arithmetic and copies ran while one was open for 4% of the time, Pallas kernels for 0%

profile of v1, /device:TPU:0, one launch (start us, length us, event | category | flops | bytes accessed | tf_op | source)
XLA Modules:
  0.0 87.3 jit_solution(11929376871455203752)
XLA Ops:
  0.0 1.0 %reshape.145 = bf16[2,1,2,8,2048]{4,3,2,0,1:T(8,128)(2,1)S(1)} reshape(bf16[2,1,2,16384]{3,2,1,0:T(2,128)(2,1)} %param.3) | data formatting | bytes 262144 | tf_op jit(solution)/shard_map/reshape | solution.py:9
  1.0 0.3 constant_dynamic-slice_fusion
  1.4 0.6 collective-permute-start
  2.0 2.6 %collective-permute-start.1 = (bf16[2,1,2,2048]{3,2,0,1:T(2,128)(2,1)S(1)}, bf16[2,1,2,2048]{3,2,0,1:T(2,128)(2,1)S(1)}, u32[]{:S(2)}, u32[]{:S(2)}) collective-permute-start(bf16[2,1,2,2048]{3,2,0,1:T(2,128)(2,1)S(1)} %bitcast.108), channel_id=1, source_target_pairs={{0,8},{4,12},{8,0},{12,4},{16,24},{20,28},{24,16},{28,20},{1,9},{5... | collective-permute-start | bytes 49160 | tf_op jit(solution)/shard_map/ppermute | solution.py:32
  4.5 0.2 collective-permute-start.2
  4.7 1.8 %collective-permute-start.3 = (bf16[2,1,2,2048]{3,2,0,1:T(2,128)(2,1)S(1)}, bf16[2,1,2,2048]{3,2,0,1:T(2,128)(2,1)S(1)}, u32[]{:S(2)}, u32[]{:S(2)}) collective-permute-start(bf16[2,1,2,2048]{3,2,0,1:T(2,128)(2,1)S(1)} %bitcast.106), channel_id=1, source_target_pairs={{0,16},{4,20},{8,24},{12,28},{16,0},{20,4},{24,8},{28,12},{1,17},{... | collective-permute-start | bytes 49160 | tf_op jit(solution)/shard_map/ppermute | solution.py:32
  6.6 0.1 collective-permute-start.4
  6.7 1.0 %reshape.143 = bf16[2,1,2,8,4,512]{5,4,3,2,0,1:T(4,128)(2,1)S(1)} reshape(bf16[2,1,2,16384]{3,2,1,0:T(2,128)(2,1)} %param.3) | data formatting | bytes 262144 | tf_op jit(solution)/shard_map/reshape | solution.py:37
  7.7 0.2 dynamic-slice_reduce_fusion
  8.0 9.4 %all_gather.3 = bf16[2,1,16,4096]{3,0,1,2:T(2,128)(2,1)S(1)} all-gather(bf16[2,1,2,4096]{3,0,1,2:T(2,128)(2,1)S(1)} %copy.18), channel_id=1, replica_groups=mesh['band'=8,'gblk'=4] {'band'}, dimensions={2}, use_global_device_ids=true | all-gather | bytes 294912 | tf_op jit(solution)/shard_map/all_gather | solution.py:54
  17.4 0.5 slice_convert_fusion.1
  17.9 0.3 copy_bitcast_fusion
  18.3 1.2 %dynamic-slice.32 = u32[1]{0:T(128)} dynamic-slice(u32[32]{0:T(128)} %constant.35, u32[]{:T(128)S(6)} %add.74), dynamic_slice_sizes={1} | dynamic-slice | bytes 12
  20.2 1.5 %collective-permute-start.5 = (bf16[2,1,2,2048]{3,2,0,1:T(2,128)(2,1)S(1)}, bf16[2,1,2,2048]{3,2,0,1:T(2,128)(2,1)S(1)}, u32[]{:S(2)}, u32[]{:S(2)}) collective-permute-start(bf16[2,1,2,2048]{3,2,0,1:T(2,128)(2,1)S(1)} %bitcast.111), channel_id=1, source_target_pairs={{0,24},{4,28},{8,16},{12,20},{16,8},{20,12},{24,0},{28,4},{1,25},{... | collective-permute-start | bytes 49160 | tf_op jit(solution)/shard_map/ppermute | solution.py:32
  21.8 1.2 %collective-permute-start.6 = (bf16[2,1,2,2048]{3,2,0,1:T(2,128)(2,1)S(1)}, bf16[2,1,2,2048]{3,2,0,1:T(2,128)(2,1)S(1)}, u32[]{:S(2)}, u32[]{:S(2)}) collective-permute-start(bf16[2,1,2,2048]{3,2,0,1:T(2,128)(2,1)S(1)} %bitcast.110), channel_id=1, source_target_pairs={{0,28},{4,24},{8,20},{12,16},{16,12},{20,8},{24,4},{28,0},{1,29},{... | collective-permute-start | bytes 49160 | tf_op jit(solution)/shard_map/ppermute | solution.py:32
  23.0 0.0 collective-permute-done.2
  23.1 1.8 %collective-permute-done.5 = bf16[2,1,2,2048]{3,2,0,1:T(2,128)(2,1)S(1)} collective-permute-done((bf16[2,1,2,2048]{3,2,0,1:T(2,128)(2,1)S(1)}, bf16[2,1,2,2048]{3,2,0,1:T(2,128)(2,1)S(1)}, u32[]{:S(2)}, u32[]{:S(2)}) %collective-permute-start.5) | collective-permute-done | bytes 16416 | tf_op jit(solution)/shard_map/ppermute | solution.py:32
  25.0 1.0 %collective-permute-done.6 = bf16[2,1,2,2048]{3,2,0,1:T(2,128)(2,1)S(1)} collective-permute-done((bf16[2,1,2,2048]{3,2,0,1:T(2,128)(2,1)S(1)}, bf16[2,1,2,2048]{3,2,0,1:T(2,128)(2,1)S(1)}, u32[]{:S(2)}, u32[]{:S(2)}) %collective-permute-start.6) | collective-permute-done | bytes 16416 | tf_op jit(solution)/shard_map/ppermute | solution.py:32
  26.0 0.8 gather_fusion
  26.8 0.1 copy.27
  26.9 0.1 reshape_reshape.3
  26.9 8.6 %fusion.2 = f32[32,4096]{1,0:T(8,128)S(1)} fusion(bf16[32,2048]{1,0:T(8,128)(2,1)S(1)} %reshape_reshape.3, bf16[2,2,4096,2048]{3,2,1,0:T(8,128)(2,1)} %bitcast.19), kind=kOutput, calls=%fused_computation.6 | convolution fusion | flops 536870912 | bytes 17432576 | tf_op jit(solution)/shard_map/dot_general | solution.py:47
  35.5 8.6 %fusion.3 = f32[32,4096]{1,0:T(8,128)S(1)} fusion(bf16[32,2048]{1,0:T(8,128)(2,1)S(1)} %reshape_reshape.3, bf16[2,2,4096,2048]{3,2,1,0:T(8,128)(2,1)} %bitcast.19), kind=kOutput, calls=%fused_computation.8 | convolution fusion | flops 536870912 | bytes 17432576 | tf_op jit(solution)/shard_map/dot_general | solution.py:44
  44.1 8.6 %fusion = f32[32,4096]{1,0:T(8,128)S(1)} fusion(bf16[32,2048]{1,0:T(8,128)(2,1)S(1)} %reshape_reshape.3, bf16[2,2,4096,2048]{3,2,1,0:T(8,128)(2,1)} %bitcast.19), kind=kOutput, calls=%fused_computation.2 | convolution fusion | flops 536870912 | bytes 17432576 | tf_op jit(solution)/shard_map/dot_general | solution.py:47
  52.7 8.6 %fusion.1 = f32[32,4096]{1,0:T(8,128)S(1)} fusion(bf16[32,2048]{1,0:T(8,128)(2,1)S(1)} %reshape_reshape.3, bf16[2,2,4096,2048]{3,2,1,0:T(8,128)(2,1)} %bitcast.19), kind=kOutput, calls=%fused_computation.4 | convolution fusion | flops 536870912 | bytes 17432576 | tf_op jit(solution)/shard_map/dot_general | solution.py:44
  61.2 0.1 fusion.10
  61.4 0.1 fusion.8
  61.5 0.2 add_reduce_fusion
  61.7 13.0 %all-reduce = f32[2,2,1,16]{3,0,2,1:T(2,128)S(1)} all-reduce(f32[2,2,1,16]{3,0,2,1:T(2,128)S(1)} %pad_maximum_fusion.1), channel_id=2, replica_groups=mesh['band'=8,'gblk'=4] {'band'}, use_global_device_ids=true, to_apply=%region_2.0.clone | all-reduce | flops 64 | bytes 512
  74.7 0.1 constant_dynamic-slice_fusion.8
  74.8 11.9 %psum.7 = f32[2,2,1,2]{3,0,2,1:T(2,128)S(1)} all-reduce(f32[2,2,1,2]{3,0,2,1:T(2,128)S(1)} %constant_dynamic-slice_fusion.8), channel_id=1, replica_groups=mesh['band'=8,'gblk'=4] {'gblk'}, use_global_device_ids=true, to_apply=%region_3.0 | all-reduce | flops 8 | bytes 64 | tf_op jit(solution)/shard_map/psum | solution.py:61
  86.7 0.6 copy.29
  (26 shorter events, 0.5 us)
Async XLA Ops:
  1.4 18.9 %collective-permute-start = (bf16[2,1,2,2048]{3,2,0,1:T(2,128)(2,1)S(1)}, bf16[2,1,2,2048]{3,2,0,1:T(2,128)(2,1)S(1)}, u32[]{:S(2)}, u32[]{:S(2)}) collective-permute-start(bf16[2,1,2,2048]{3,2,0,1:T(2,128)(2,1)S(1)} %bitcast.109), channel_id=1, source_target_pairs={{0,4},{4,0},{8,12},{12,8},{16,20},{20,16},{24,28},{28,24},{1,5},{5... | collective-permute-start | bytes 49160 | tf_op jit(solution)/shard_map/ppermute | solution.py:32
  2.0 19.8 %collective-permute-start.1 = (bf16[2,1,2,2048]{3,2,0,1:T(2,128)(2,1)S(1)}, bf16[2,1,2,2048]{3,2,0,1:T(2,128)(2,1)S(1)}, u32[]{:S(2)}, u32[]{:S(2)}) collective-permute-start(bf16[2,1,2,2048]{3,2,0,1:T(2,128)(2,1)S(1)} %bitcast.108), channel_id=1, source_target_pairs={{0,8},{4,12},{8,0},{12,4},{16,24},{20,28},{24,16},{28,20},{1,9},{5... | collective-permute-start | bytes 49160 | tf_op jit(solution)/shard_map/ppermute | solution.py:32
  4.5 18.5 %collective-permute-start.2 = (bf16[2,1,2,2048]{3,2,0,1:T(2,128)(2,1)S(1)}, bf16[2,1,2,2048]{3,2,0,1:T(2,128)(2,1)S(1)}, u32[]{:S(2)}, u32[]{:S(2)}) collective-permute-start(bf16[2,1,2,2048]{3,2,0,1:T(2,128)(2,1)S(1)} %bitcast.107), channel_id=1, source_target_pairs={{0,12},{4,8},{8,4},{12,0},{16,28},{20,24},{24,20},{28,16},{1,13},{... | collective-permute-start | bytes 49160 | tf_op jit(solution)/shard_map/ppermute | solution.py:32
  4.7 18.3 %collective-permute-start.3 = (bf16[2,1,2,2048]{3,2,0,1:T(2,128)(2,1)S(1)}, bf16[2,1,2,2048]{3,2,0,1:T(2,128)(2,1)S(1)}, u32[]{:S(2)}, u32[]{:S(2)}) collective-permute-start(bf16[2,1,2,2048]{3,2,0,1:T(2,128)(2,1)S(1)} %bitcast.106), channel_id=1, source_target_pairs={{0,16},{4,20},{8,24},{12,28},{16,0},{20,4},{24,8},{28,12},{1,17},{... | collective-permute-start | bytes 49160 | tf_op jit(solution)/shard_map/ppermute | solution.py:32
  6.6 16.5 %collective-permute-start.4 = (bf16[2,1,2,2048]{3,2,0,1:T(2,128)(2,1)S(1)}, bf16[2,1,2,2048]{3,2,0,1:T(2,128)(2,1)S(1)}, u32[]{:S(2)}, u32[]{:S(2)}) collective-permute-start(bf16[2,1,2,2048]{3,2,0,1:T(2,128)(2,1)S(1)} %bitcast.105), channel_id=1, source_target_pairs={{0,20},{4,16},{8,28},{12,24},{16,4},{20,0},{24,12},{28,8},{1,21},{... | collective-permute-start | bytes 49160 | tf_op jit(solution)/shard_map/ppermute | solution.py:32
  20.2 4.7 %collective-permute-start.5 = (bf16[2,1,2,2048]{3,2,0,1:T(2,128)(2,1)S(1)}, bf16[2,1,2,2048]{3,2,0,1:T(2,128)(2,1)S(1)}, u32[]{:S(2)}, u32[]{:S(2)}) collective-permute-start(bf16[2,1,2,2048]{3,2,0,1:T(2,128)(2,1)S(1)} %bitcast.111), channel_id=1, source_target_pairs={{0,24},{4,28},{8,16},{12,20},{16,8},{20,12},{24,0},{28,4},{1,25},{... | collective-permute-start | bytes 49160 | tf_op jit(solution)/shard_map/ppermute | solution.py:32
  21.8 4.1 %collective-permute-start.6 = (bf16[2,1,2,2048]{3,2,0,1:T(2,128)(2,1)S(1)}, bf16[2,1,2,2048]{3,2,0,1:T(2,128)(2,1)S(1)}, u32[]{:S(2)}, u32[]{:S(2)}) collective-permute-start(bf16[2,1,2,2048]{3,2,0,1:T(2,128)(2,1)S(1)} %bitcast.110), channel_id=1, source_target_pairs={{0,28},{4,24},{8,20},{12,16},{16,12},{20,8},{24,4},{28,0},{1,29},{... | collective-permute-start | bytes 49160 | tf_op jit(solution)/shard_map/ppermute | solution.py:32
